TPU v7x, 8 devices: a whole 2x2x1 slice. The times are simulated.
8 devices in a mesh: dp: 2 (over y, z), tp: 4 (over x, core).
Axes of the slice: x: 2, y: 2, z: 1, core: 2. Of those that a mesh axis runs over, the one named last changes fastest.
Arguments:
- x: bfloat16 [1536, 6144], P(('dp', 'tp')), parts along dimension 0
- w_gate: bfloat16 [6144, 16384], P(None, 'tp')
- w_up: bfloat16 [6144, 16384], P(None, 'tp')
- w_down: bfloat16 [16384, 6144], P('tp')
Outputs:
- output: bfloat16 [1536, 6144], P(('dp', 'tp')), parts along dimension 0
There are 2 independent parts. A program takes and returns all parts, laid end to end along the dimension named above; an argument that names none is the same for every part.
All inputs are finite; a program needn't handle non-finite values.
Results may differ from a plain program's by a relative error of at most 0.016.
Values are sent between devices in bfloat16 or wider.
A program may use at most 2 GiB of HBM per device.

v0:
```python
import jax
import jax.numpy as jnp
from jax import lax
from jax.sharding import PartitionSpec as P


def solution(mesh):
    def step(x, w_gate, w_up, w_down):
        rows = lax.all_gather(x, "tp", axis=0, tiled=True)
        gate = jnp.dot(rows, w_gate, preferred_element_type=jnp.float32)
        up = jnp.dot(rows, w_up, preferred_element_type=jnp.float32)
        hidden = (jax.nn.silu(gate) * up).astype(jnp.bfloat16)
        term = jnp.dot(hidden, w_down, preferred_element_type=jnp.float32).astype(jnp.bfloat16)
        return lax.psum_scatter(term, "tp", scatter_dimension=0, tiled=True)

    return jax.shard_map(
        step,
        mesh=mesh,
        in_specs=(P(("dp", "tp"), None), P(None, "tp"), P(None, "tp"), P("tp", None)),
        out_specs=P(("dp", "tp"), None),
        check_vma=False,
    )
```

profile of v0, /device:TPU:0, one launch (start us, length us, event | category | flops | bytes accessed | tf_op | source)
XLA Modules:
  0.0 294.2 jit_solution(16152669647257540801)
XLA Ops:
  6.5 0.0 all-gather.2.cloned.1.call-start
  6.5 0.7 all-gather.2.cloned.1.call-update
  7.3 0.0 reduce-scatter.2.cloned.1.call-start
  7.3 66.2 %all-gather.2.cloned.1.call-done = bf16[768,6144]{1,0:T(8,128)(2,1)} async-done(((bf16[192,6144]{1,0:T(8,128)(2,1)}), bf16[768,6144]{1,0:T(8,128)(2,1)}) %all-gather.2.cloned.1.call-update) | async-done | bytes 9437200 | tf_op jit(solution)/shard_map/all_gather | solution.py:9
  73.5 0.0 copy-start
  73.5 51.8 %fusion = f32[768,4096]{1,0:T(8,128)} fusion(bf16[768,6144]{1,0:T(8,128)(2,1)} %all-gather.2.cloned.1.call-done, bf16[6144,4096]{1,0:T(8,128)(2,1)} %param.5), kind=kOutput, calls=%fused_computation.2 | convolution fusion | flops 38654705664 | bytes 72351744 | tf_op jit(solution)/shard_map/dot_general | solution.py:10
  125.3 0.0 copy-done
  125.3 45.1 %multiply_convert_fusion = bf16[768,4096]{1,0:T(8,128)(2,1)S(1)} fusion(f32[768,4096]{1,0:T(8,128)} %fusion, bf16[768,6144]{1,0:T(8,128)(2,1)S(1)} %copy-done, bf16[6144,4096]{1,0:T(8,128)(2,1)} %param.6), kind=kOutput, calls=%fused_computation | convolution fusion | flops 38673580032 | bytes 78643200 | tf_op jit(solution)/shard_map/dot_general | solution.py:11
  170.5 45.2 %convolution_convert_fusion = bf16[768,6144]{1,0:T(8,128)(2,1)} fusion(bf16[768,4096]{1,0:T(8,128)(2,1)S(1)} %multiply_convert_fusion, bf16[4096,6144]{1,0:T(8,128)(2,1)} %param.7), kind=kOutput, calls=%fused_computation.1 | convolution fusion | flops 38659424256 | bytes 66060288 | tf_op jit(solution)/shard_map/dot_general | solution.py:13
  215.6 0.0 reduce-scatter.2.cloned.1.call-update
  215.7 71.7 %reduce-scatter.2.cloned.1.call-done = bf16[192,6144]{1,0:T(8,128)(2,1)} async-done(((bf16[768,6144]{1,0:T(8,128)(2,1)}), bf16[192,6144]{1,0:T(8,128)(2,1)}) %reduce-scatter.2.cloned.1.call-update) | async-done | bytes 2359312 | tf_op jit(solution)/shard_map/reduce_scatter | solution.py:14
Async XLA Ops:
  6.5 67.0 %all-gather.2.cloned.1.call-start = ((), (), s32[]{:S(2)}) async-start(), calls=%async_computation.1 | async-start | bytes 11796480 | tf_op jit(solution)/shard_map/all_gather | solution.py:9
  7.3 280.1 %reduce-scatter.2.cloned.1.call-start = ((), (), s32[]{:S(2)}) async-start(), calls=%async_computation.2 | async-start | bytes 11796480 | tf_op jit(solution)/shard_map/reduce_scatter | solution.py:14
  73.5 51.8 %copy-start = (bf16[768,6144]{1,0:T(8,128)(2,1)S(1)}, bf16[768,6144]{1,0:T(8,128)(2,1)}, u32[]{:S(2)}) copy-start(bf16[768,6144]{1,0:T(8,128)(2,1)} %all-gather.2.cloned.1.call-done) | copy-start | bytes 28311556
Sparse Core Ops, SparseCore 0:
  8.9 64.5 all-gather.1
  215.8 71.4 reduce-scatter.1
where the time goes:
time: 294 us
  matrix products  142 us (48%)
  waiting for transfers between devices  139 us (47%)
  between operations  13.4 us (5%)
    reduce_scatter x1, waiting for transfers between devices, step(): return lax.psum_scatter(term, 'tp', scatter_dimension=0, tiled=True)  71.7 us
    all_gather x1, waiting for transfers between devices, step(): rows = lax.all_gather(x, 'tp', axis=0, tiled=True)  66.2 us
    dot_general x1, matrix products, step(): gate = jnp.dot(rows, w_gate, preferred_element_type=jnp.float32)  51.8 us
    dot_general x1, matrix products, step(): jnp.dot(hidden, w_down, preferred_element_type=jnp.float32)  45.2 us
    dot_general x1, matrix products, step(): up = jnp.dot(rows, w_up, preferred_element_type=jnp.float32)  45.1 us
  transfers between devices with their start and end apart: 2, of which 2 were waited for; matrix products, arithmetic and copies ran while one was open for 0% of the time, Pallas kernels for 0%

commit v1 on v0

v1 whole, which is shorter than its diff:
```python
import jax
import jax.numpy as jnp
from jax import lax
from jax.experimental import pallas as pl
from jax.experimental.pallas import tpu as pltpu
from jax.sharding import PartitionSpec as P

D = 6144
F = 4096
R = 192
H2 = R // 2
NB = 512
ND = D // NB
NI = F // 512
BF = jnp.bfloat16
F32 = jnp.float32
MESH = pl.DeviceIdType.MESH
CHUNK = 48
NCH = R // CHUNK


def kernel(x_hbm, wg, wu, wd, out_hbm, X, H, W, rD, rR, rP, O, T,
           wsem, lsem, ps, pr, xs, xr, ys, yr, ds_, dr, rs, rr, qs, qr, osem):
    me = lax.axis_index("tp")
    partner = me + 1 - 2 * lax.rem(me, 2)
    remote = lax.rem(me + 2, 4)

    def rcopy(src, dst, s, r, dev):
        return pltpu.make_async_remote_copy(
            src_ref=src, dst_ref=dst, send_sem=s, recv_sem=r,
            device_id={"tp": dev}, device_id_type=MESH)

    def load_own(c):
        rows = pl.ds(c * H2, H2)
        return pltpu.make_async_copy(x_hbm.at[rows, :], X.at[rows, :], lsem.at[c])

    def to_partner(c):
        return rcopy(X.at[pl.ds(c * H2, H2), :], X.at[pl.ds(R + c * H2, H2), :],
                     ps.at[c], pr.at[c], partner)

    def far_row(k, diag):
        half, inside = (k * CHUNK) // H2, (k * CHUNK) % H2
        return 2 * R + half * R + diag * H2 + inside

    def to_remote(k):
        return rcopy(X.at[pl.ds(k * CHUNK, CHUNK), :], X.at[pl.ds(far_row(k, 0), CHUNK), :],
                     xs.at[k], xr.at[k], remote)

    def relay(k):
        return rcopy(X.at[pl.ds(far_row(k, 0), CHUNK), :], X.at[pl.ds(far_row(k, 1), CHUNK), :],
                     ys.at[k], yr.at[k], partner)

    def gu_copies(i, slot):
        out = []
        for b in range(2):
            col = pl.multiple_of(i * 512 + b * 256, 256)
            for q, w in ((0, wg), (1, wu)):
                out.append(pltpu.make_async_copy(
                    w.at[:, pl.ds(col, 256)],
                    W.at[slot, :, pl.ds(b * 512 + q * 256, 256)],
                    wsem.at[slot, 2 * b + q]))
        return out

    def dn_copy(q):
        slot = lax.rem(q + 1, 2)
        col = pl.multiple_of(lax.rem(q, ND) * NB, NB)
        return pltpu.make_async_copy(
            wd.at[:, pl.ds(col, NB)], W.at[slot, pl.ds(0, F), pl.ds(0, NB)], wsem.at[slot, 0])

    def gu(rows, m, slot, i):
        for b in range(2):
            r = jnp.dot(X[pl.ds(rows, m), :], W[slot, :, pl.ds(b * 512, 512)],
                        preferred_element_type=F32)
            col = pl.multiple_of(i * 512 + b * 256, 256)
            H[pl.ds(rows, m), pl.ds(col, 256)] = (jax.nn.silu(r[:, :256]) * r[:, 256:]).astype(BF)

    for c in range(2):
        load_own(c).start()
    for c in gu_copies(0, 0):
        c.start()

    barrier = pltpu.get_barrier_semaphore()
    for dev in (partner, remote):
        pl.semaphore_signal(barrier, inc=1, device_id={"tp": dev}, device_id_type=MESH)
    pl.semaphore_wait(barrier, 2)
    for c in range(2):
        load_own(c).wait()
        to_partner(c).start()
        for k in range(c * NCH // 2, (c + 1) * NCH // 2):
            to_remote(k).start()

    for c in gu_copies(1, 1):
        c.start()
    for c in gu_copies(0, 0):
        c.wait()
    gu(0, R, 0, 0)
    for c in range(2):
        to_partner(c).wait_recv()
    gu(R, R, 0, 0)

    def first(t, carry):
        slot = lax.rem(t, 2)
        for c in gu_copies(t, slot):
            c.wait()
        for c in gu_copies(t + 1, 1 - slot):
            c.start()

        @pl.when(t == 3)
        def _():
            to_remote(0).wait_recv()
            relay(0).start()

        gu(0, 2 * R, slot, t)
        return carry

    lax.fori_loop(1, 5, first, 0)

    def second(t, carry):
        slot = lax.rem(t, 2)
        for c in gu_copies(t, slot):
            c.wait()

        @pl.when(t < NI - 1)
        def _():
            for c in gu_copies(t + 1, 1 - slot):
                c.start()

        @pl.when(t == 5)
        def _():
            to_remote(1).wait_recv()
            relay(1).start()

        @pl.when(t == 7)
        def _():
            to_remote(2).wait_recv()
            relay(2).start()

        gu(0, 2 * R, slot, t)

        @pl.when(t == 5)
        def _():
            relay(0).wait_recv()
            relay(1).wait_recv()

        gu(2 * R, R, slot, t)
        return carry

    lax.fori_loop(5, NI, second, 0)

    to_remote(3).wait_recv()
    relay(3).start()
    relay(2).wait_recv()
    relay(3).wait_recv()

    def third(k, carry):
        i = NI - 1 - k
        slot = lax.rem(i, 2)

        @pl.when(k >= 2)
        def _():
            for c in gu_copies(i, slot):
                c.wait()

        @pl.when(k >= 1)
        def _():
            for c in gu_copies(i - 1, 1 - slot):
                c.start()

        gu(3 * R, R, slot, i)
        return carry

    lax.fori_loop(0, 3, third, 0)

    def fourth(k, carry):
        i = NI - 1 - k
        slot = lax.rem(i, 2)
        for c in gu_copies(i, slot):
            c.wait()

        @pl.when(i >= 1)
        def _():
            for c in gu_copies(i - 1, 1 - slot):
                c.start()

        @pl.when(i == 0)
        def _():
            dn_copy(0).start()

        gu(2 * R, 2 * R, slot, i)
        return carry

    lax.fori_loop(3, NI, fourth, 0)

    for c in range(2):
        to_partner(c).wait_send()
    for k in range(NCH):
        to_remote(k).wait_send()
        relay(k).wait_send()

    def cols(n):
        return pl.ds(pl.multiple_of(n * NB, NB), NB)

    def send_d(n):
        return rcopy(X.at[pl.ds(0, R), cols(n)], rD.at[:, cols(n)], ds_.at[n], dr.at[n], partner)

    def send_r(n):
        return rcopy(X.at[pl.ds(R, R), cols(n)], rR.at[:, cols(n)], rs.at[n], rr.at[n], remote)

    def send_p(n):
        return rcopy(X.at[pl.ds(2 * R, R), cols(n)], rP.at[:, cols(n)], qs.at[n], qr.at[n], partner)

    def store_out(n):
        return pltpu.make_async_copy(X.at[pl.ds(3 * R, R), cols(n)], out_hbm.at[:, cols(n)], osem.at[n])

    def pair_sum(n):
        send_d(n).wait_recv()
        X[pl.ds(R, R), cols(n)] = (
            T[lax.rem(n, 2)] + rD[:, cols(n)].astype(F32)).astype(BF)

    def far(n, carry):
        slot = lax.rem(n + 1, 2)
        dn_copy(n).wait()
        dn_copy(n + 1).start()

        @pl.when(n >= 1)
        def _():
            send_d(n - 1).start()

        @pl.when(n >= 2)
        def _():
            send_r(n - 2).start()

        r = jnp.dot(H[pl.ds(2 * R, 2 * R), :], W[slot, pl.ds(0, F), pl.ds(0, NB)],
                    preferred_element_type=F32)
        p = lax.rem(n, 2)
        for h in range(2):
            T[p, pl.ds(h * H2, H2), :] = r[h * R:h * R + H2]
            X[pl.ds(h * H2, H2), cols(n)] = r[h * R + H2:(h + 1) * R].astype(BF)

        @pl.when(n >= 1)
        def _():
            pair_sum(n - 1)

        return carry

    lax.fori_loop(0, ND, far, 0)

    def near(n, carry):
        slot = lax.rem(n + 1, 2)
        dn_copy(ND + n).wait()

        @pl.when(n < ND - 1)
        def _():
            dn_copy(ND + n + 1).start()

        @pl.when(n == 0)
        def _():
            send_d(ND - 1).start()

        @pl.when(n < 2)
        def _():
            send_r(ND - 2 + n).start()

        @pl.when(n >= 1)
        def _():
            send_p(n - 1).start()

        r = jnp.dot(H[pl.ds(0, 2 * R), :], W[slot, pl.ds(0, F), pl.ds(0, NB)],
                    preferred_element_type=F32)
        O[:, cols(n)] = r[:R]
        X[pl.ds(2 * R, R), cols(n)] = r[R:].astype(BF)

        @pl.when(n == 0)
        def _():
            pair_sum(ND - 1)

        return carry

    lax.fori_loop(0, ND, near, 0)
    send_p(ND - 1).start()

    def finish(n, carry):
        send_p(n).wait_recv()
        send_r(n).wait_recv()
        X[pl.ds(3 * R, R), cols(n)] = (
            O[:, cols(n)] + rP[:, cols(n)].astype(F32) + rR[:, cols(n)].astype(F32)).astype(BF)

        @pl.when(n >= 1)
        def _():
            store_out(n - 1).start()

        return carry

    lax.fori_loop(0, ND, finish, 0)

    def drain(n, carry):
        send_d(n).wait_send()
        send_r(n).wait_send()
        send_p(n).wait_send()
        return carry

    lax.fori_loop(0, ND, drain, 0)
    store_out(ND - 1).start()

    def stored(n, carry):
        store_out(n).wait()
        return carry

    lax.fori_loop(0, ND, stored, 0)


def solution(mesh):
    dma = pltpu.SemaphoreType.DMA

    def step(x, w_gate, w_up, w_down):
        hbm = pl.BlockSpec(memory_space=pl.ANY)
        return pl.pallas_call(
            kernel,
            out_shape=jax.ShapeDtypeStruct((R, D), BF),
            in_specs=[hbm] * 4,
            out_specs=hbm,
            scratch_shapes=[
                pltpu.VMEM((4 * R, D), BF),
                pltpu.VMEM((4 * R, F), BF),
                pltpu.VMEM((2, D, 1024), BF),
                pltpu.VMEM((R, D), BF),
                pltpu.VMEM((R, D), BF),
                pltpu.VMEM((R, D), BF),
                pltpu.VMEM((R, D), F32),
                pltpu.VMEM((2, R, NB), F32),
                dma((2, 4)), dma((2,)),
                dma((2,)), dma((2,)),
                dma((NCH,)), dma((NCH,)),
                dma((NCH,)), dma((NCH,)),
                dma((ND,)), dma((ND,)),
                dma((ND,)), dma((ND,)),
                dma((ND,)), dma((ND,)),
                dma((ND,)),
            ],
            compiler_params=pltpu.CompilerParams(
                collective_id=0, has_side_effects=True, vmem_limit_bytes=66 * 2**20 - 2**21 - 2**17),
            name="mlp",
        )(x, w_gate, w_up, w_down)

    return jax.shard_map(
        step,
        mesh=mesh,
        in_specs=(P(("dp", "tp"), None), P(None, "tp"), P(None, "tp"), P("tp", None)),
        out_specs=P(("dp", "tp"), None),
        check_vma=False,
    )
```

time: 294 us -> 159 us (0.54)
  Pallas kernels: 0 us -> 154 us
  matrix products: 142 us -> 0 us
  waiting for transfers between devices: 139 us -> 0 us
  between operations: 13.4 us -> 0.01 us
  local copies, waits for them, and re-layouts: 0.01 us -> 3.3 us
    pallas_call x0 -> x1, Pallas kernels: none -> 154 us  [step(): pl.pallas_call(kernel, out_shape=jax.ShapeDtypeStruct((R, D), BF), in_spe...]
    dot_general x3 -> x0, matrix products: 142 us -> none  [the longest x1 51.8 us: step(): gate = jnp.dot(rows, w_gate, preferred_element_type=jnp.float32)]
    reduce_scatter x1 -> x0, waiting for transfers between devices: 71.7 us -> none  [step(): return lax.psum_scatter(term, 'tp', scatter_dimension=0, tiled=True)]
    all_gather x1 -> x0, waiting for transfers between devices: 66.2 us -> none  [step(): rows = lax.all_gather(x, 'tp', axis=0, tiled=True)]
    unnamed x2 -> x1, local copies, waits for them, and re-layouts: 0.01 us -> 3.3 us
  transfers between devices with their start and end apart: 2 -> 0, of which waited for: 2 -> 0; matrix products, arithmetic and copies ran while one was open for 0% -> 0% of each run, Pallas kernels for 0% -> 0%
where the time goes in v1:
time: 159 us; the launch traced here: 158 us
  Pallas kernels  154 us (97%)
  local copies, waits for them, and re-layouts  3.3 us (2%)
    pallas_call x1, Pallas kernels, step(): pl.pallas_call(kernel, out_shape=jax.ShapeDtypeStruct((R, D), BF), in_spe...  154 us
    unnamed x1, local copies, waits for them, and re-layouts  3.3 us

profile of v1, /device:TPU:0, one launch (start us, length us, event | category | flops | bytes accessed | tf_op | source)
XLA Modules:
  0.0 157.7 jit_solution(14943261600519538218)
XLA Ops:
  0.0 154.4 %mlp.1 = bf16[192,6144]{1,0:T(8,128)(2,1)} custom-call(bf16[192,6144]{1,0:T(8,128)(2,1)} %x_hbm.1, bf16[6144,4096]{1,0:T(8,128)(2,1)} %wg.1, bf16[6144,4096]{1,0:T(8,128)(2,1)} %wu.1, bf16[4096,6144]{1,0:T(8,128)(2,1)} %wd.1), custom_call_target="tpu_custom_call" | custom-call | tf_op jit(solution)/shard_map/mlp/pallas_call | solution.py:317
  154.4 3.3 %copy.6 = bf16[192,6144]{1,0:T(8,128)(2,1)} copy(bf16[192,6144]{1,0:T(8,128)(2,1)} %mlp.1) | data formatting | bytes 4718592

commit v2 on v0

v2 whole, which is shorter than its diff:
```python
import jax
import jax.numpy as jnp
from jax import lax
from jax.experimental import pallas as pl
from jax.experimental.pallas import tpu as pltpu
from jax.sharding import PartitionSpec as P

D = 6144
F = 4096
R = 192
KH = D // 2
NB = 512
ND = D // NB
BF = jnp.bfloat16
F32 = jnp.float32
MESH = pl.DeviceIdType.MESH
CHUNKS = ((0, 1536), (1536, 1536), (3072, 1536), (4608, 1024), (5632, 512))
NCH = len(CHUNKS)

T_K = 7
T_FAR = T_K + 8
T_LAST = T_FAR + ND
T_NEAR = T_LAST + 1
T_END = T_NEAR + ND


def kernel(x_hbm, wg, wu, wd, out, X, H, W, S, rD, rR, rP,
           wsem, lsem, ps, pr, xs, xr, ys, yr, ds_, dr, rs, rr, qs, qr):
    me = lax.axis_index("tp")
    partner = me + 1 - 2 * lax.rem(me, 2)
    remote = lax.rem(me + 2, 4)

    def rcopy(src, dst, s, r, dev):
        return pltpu.make_async_remote_copy(
            src_ref=src, dst_ref=dst, send_sem=s, recv_sem=r,
            device_id={"tp": dev}, device_id_type=MESH)

    def load_own():
        return pltpu.make_async_copy(x_hbm, X.at[pl.ds(0, R), :], lsem)

    def to_partner(c):
        rows = R // 2
        return rcopy(x_hbm.at[pl.ds(c * rows, rows), :], X.at[pl.ds(R + c * rows, rows), :],
                     ps.at[c], pr.at[c], partner)

    def to_remote(k):
        c = pl.ds(*CHUNKS[k])
        return rcopy(x_hbm.at[:, c], X.at[pl.ds(2 * R, R), c], xs.at[k], xr.at[k], remote)

    def relay(k):
        c = pl.ds(*CHUNKS[k])
        return rcopy(X.at[pl.ds(2 * R, R), c], X.at[pl.ds(3 * R, R), c], ys.at[k], yr.at[k], partner)

    def own_copies(i, slot, halves=(0, 1)):
        out = []
        for b in halves:
            col = pl.multiple_of(i * 512 + b * 256, 256)
            for q, w in ((0, wg), (1, wu)):
                out.append(pltpu.make_async_copy(
                    w.at[:, pl.ds(col, 256)],
                    W.at[slot, :, pl.ds(b * 512 + q * 256, 256)],
                    wsem.at[slot, 2 * b + q]))
        return out

    def half_copies(j, slot):
        row = pl.multiple_of((j // 4) * KH, KH)
        out = []
        for b in range(4):
            col = pl.multiple_of(lax.rem(j, 4) * 1024 + b * 256, 256)
            for q, w in ((0, wg), (1, wu)):
                out.append(pltpu.make_async_copy(
                    w.at[pl.ds(row, KH), pl.ds(col, 256)],
                    W.at[slot, pl.ds(b // 2 * KH, KH), pl.ds(b % 2 * 512 + q * 256, 256)],
                    wsem.at[slot, 2 * b + q]))
        return out

    def down_copies(n, slot):
        col = pl.multiple_of(n * NB, NB)
        return [pltpu.make_async_copy(
            wd.at[:, pl.ds(col, NB)], W.at[slot, pl.ds(0, F), pl.ds(0, NB)], wsem.at[slot, 0])]

    def own_block(t):
        return t - (T_LAST - T_K) * (t // T_LAST)

    def down_block(t):
        return t - T_FAR - (ND + 1) * (t // T_NEAR)

    is_own = lambda t: (t < T_K) | (t == T_LAST)
    is_half = lambda t: (t >= T_K) & (t < T_FAR)
    is_down = lambda t: (t >= T_FAR) & (t != T_LAST)

    def start_weights(t):
        slot = lax.rem(t, 2)

        @pl.when(is_own(t))
        def _():
            for c in own_copies(own_block(t), slot):
                c.start()

        @pl.when(is_half(t))
        def _():
            for c in half_copies(t - T_K, slot):
                c.start()

        @pl.when(is_down(t))
        def _():
            for c in down_copies(down_block(t), slot):
                c.start()

    def cols(n):
        return pl.ds(pl.multiple_of(n * NB, NB), NB)

    def hidden(i, b):
        return pl.ds(pl.multiple_of(i * 512 + b * 256, 256), 256)

    def act(r):
        return (jax.nn.silu(r[:, :256]) * r[:, 256:]).astype(BF)

    def own(rows, m, slot, i, b):
        r = jnp.dot(X[pl.ds(rows, m), :], W[slot, :, pl.ds(b * 512, 512)],
                    preferred_element_type=F32)
        H[pl.ds(rows, m), hidden(i, b)] = act(r)

    def far_half(half, slot, c, b):
        return jnp.dot(X[pl.ds(2 * R, 2 * R), pl.ds(half * KH, KH)],
                       W[slot, pl.ds(b // 2 * KH, KH), pl.ds(b % 2 * 512, 512)],
                       preferred_element_type=F32)

    def part(c, b):
        return pl.ds(pl.multiple_of(c * 2048 + b * 512, 512), 512)

    load_own().start()
    for c in own_copies(0, 0):
        c.start()

    barrier = pltpu.get_barrier_semaphore()
    for dev in (partner, remote):
        pl.semaphore_signal(barrier, inc=1, device_id={"tp": dev}, device_id_type=MESH)
    pl.semaphore_wait(barrier, 2)
    to_remote(0).start()
    for c in range(2):
        to_partner(c).start()
    for k in range(1, NCH):
        to_remote(k).start()

    for c in own_copies(1, 1):
        c.start()
    load_own().wait()
    for b in range(2):
        for c in own_copies(0, 0, (b,)):
            c.wait()
        own(0, R, 0, 0, b)
    for c in range(2):
        to_partner(c).wait_recv()
    for b in range(2):
        own(R, R, 0, 0, b)

    def send_d(n):
        return rcopy(X.at[pl.ds(2 * R, R), cols(n)], rD.at[:, cols(n)], ds_.at[n], dr.at[n], partner)

    def send_r(n):
        return rcopy(X.at[pl.ds(3 * R, R), cols(n)], rR.at[:, cols(n)], rs.at[n], rr.at[n], remote)

    def send_p(n):
        return rcopy(X.at[pl.ds(0, R), cols(n)], rP.at[:, cols(n)], qs.at[n], qr.at[n], partner)

    def held(n):
        return pl.ds(pl.multiple_of(lax.rem(n, 2) * NB, NB), NB)

    def step(t, carry):
        slot = lax.rem(t, 2)

        @pl.when(is_own(t))
        def _():
            for c in own_copies(own_block(t), slot):
                c.wait()

        @pl.when(is_half(t))
        def _():
            for c in half_copies(t - T_K, slot):
                c.wait()

        @pl.when(is_down(t))
        def _():
            for c in down_copies(down_block(t), slot):
                c.wait()

        @pl.when(t < T_END - 1)
        def _():
            start_weights(t + 1)

        for k, when in enumerate((4, 6, 9, 10, T_K + 4)):
            @pl.when(t == when)
            def _(k=k):
                to_remote(k).wait_recv()
                relay(k).start()

        @pl.when(t == T_K)
        def _():
            for k in (0, 1):
                relay(k).wait_recv()

        @pl.when(t == T_K + 4)
        def _():
            for k in (2, 3, 4):
                relay(k).wait_recv()

        @pl.when(t == T_FAR)
        def _():
            for c in range(2):
                to_partner(c).wait_send()
            for k in range(NCH):
                to_remote(k).wait_send()
                relay(k).wait_send()

        @pl.when((t > T_FAR) & (t <= T_LAST))
        def _():
            send_d(t - T_FAR - 1).start()

        @pl.when((t > T_FAR + 1) & (t <= T_NEAR))
        def _():
            send_r(t - T_FAR - 2).start()

        @pl.when(t > T_NEAR)
        def _():
            send_p(t - T_NEAR - 1).start()

        @pl.when(is_own(t))
        def _():
            for b in range(2):
                own(0, 2 * R, slot, own_block(t), b)

        @pl.when((t >= T_K) & (t < T_K + 4))
        def _():
            c = t - T_K
            for b in range(4):
                S[:, part(c, b)] = far_half(0, slot, c, b)

        @pl.when((t >= T_K + 4) & (t < T_FAR))
        def _():
            c = t - T_K - 4
            for b in range(4):
                r = far_half(1, slot, c, b) + S[:, part(c, b)]
                H[pl.ds(2 * R, 2 * R), hidden(2 * c + b // 2, b % 2)] = act(r)

        @pl.when((t >= T_FAR) & (t < T_LAST))
        def _():
            n = t - T_FAR
            r = jnp.dot(H[pl.ds(2 * R, 2 * R), :], W[slot, pl.ds(0, F), pl.ds(0, NB)],
                        preferred_element_type=F32)
            S[pl.ds(R, R), held(n)] = r[:R]
            X[pl.ds(2 * R, R), cols(n)] = r[R:].astype(BF)

        @pl.when(t >= T_NEAR)
        def _():
            n = t - T_NEAR
            r = jnp.dot(H[pl.ds(0, 2 * R), :], W[slot, pl.ds(0, F), pl.ds(0, NB)],
                        preferred_element_type=F32)
            S[pl.ds(0, R), cols(n)] = r[:R]
            X[pl.ds(0, R), cols(n)] = r[R:].astype(BF)

        @pl.when((t > T_FAR) & (t <= T_LAST))
        def _():
            n = t - T_FAR - 1
            send_d(n).wait_recv()
            X[pl.ds(3 * R, R), cols(n)] = (
                S[pl.ds(R, R), held(n)] + rD[:, cols(n)].astype(F32)).astype(BF)

        return carry

    lax.fori_loop(1, T_END, step, 0)
    send_p(ND - 1).start()

    def finish(n, carry):
        send_p(n).wait_recv()
        send_r(n).wait_recv()
        out[:, cols(n)] = (S[pl.ds(0, R), cols(n)] + rP[:, cols(n)].astype(F32)
                           + rR[:, cols(n)].astype(F32)).astype(BF)
        return carry

    lax.fori_loop(0, ND, finish, 0)

    def drain(n, carry):
        send_d(n).wait_send()
        send_r(n).wait_send()
        send_p(n).wait_send()
        return carry

    lax.fori_loop(0, ND, drain, 0)


def solution(mesh):
    dma = pltpu.SemaphoreType.DMA

    def step(x, w_gate, w_up, w_down):
        hbm = pl.BlockSpec(memory_space=pl.ANY)
        return pl.pallas_call(
            kernel,
            out_shape=pltpu.VMEM((R, D), BF),
            in_specs=[hbm] * 4,
            out_specs=pl.BlockSpec(memory_space=pltpu.VMEM),
            scratch_shapes=[
                pltpu.VMEM((4 * R, D), BF),
                pltpu.VMEM((4 * R, F), BF),
                pltpu.VMEM((2, D, 1024), BF),
                pltpu.VMEM((2 * R, 2 * F), F32),
                pltpu.VMEM((R, D), BF),
                pltpu.VMEM((R, D), BF),
                pltpu.VMEM((R, D), BF),
                dma((2, 8)), dma,
                dma((2,)), dma((2,)),
                dma((NCH,)), dma((NCH,)),
                dma((NCH,)), dma((NCH,)),
                dma((ND,)), dma((ND,)),
                dma((ND,)), dma((ND,)),
                dma((ND,)), dma((ND,)),
            ],
            compiler_params=pltpu.CompilerParams(
                collective_id=0, has_side_effects=True, vmem_limit_bytes=64500000),
            name="mlp",
        )(x, w_gate, w_up, w_down)

    return jax.shard_map(
        step,
        mesh=mesh,
        in_specs=(P(("dp", "tp"), None), P(None, "tp"), P(None, "tp"), P("tp", None)),
        out_specs=P(("dp", "tp"), None),
        check_vma=False,
    )
```

time: 294 us -> 149 us (0.51)
  Pallas kernels: 0 us -> 147 us
  matrix products: 142 us -> 0 us
  waiting for transfers between devices: 139 us -> 0 us
  between operations: 13.4 us -> 0.01 us
    pallas_call x0 -> x1, Pallas kernels: none -> 147 us  [step(): pl.pallas_call(kernel, out_shape=pltpu.VMEM((R, D), BF), in_specs=[hbm] *...]
    dot_general x3 -> x0, matrix products: 142 us -> none  [the longest x1 51.8 us: step(): gate = jnp.dot(rows, w_gate, preferred_element_type=jnp.float32)]
    reduce_scatter x1 -> x0, waiting for transfers between devices: 71.7 us -> none  [step(): return lax.psum_scatter(term, 'tp', scatter_dimension=0, tiled=True)]
    all_gather x1 -> x0, waiting for transfers between devices: 66.2 us -> none  [step(): rows = lax.all_gather(x, 'tp', axis=0, tiled=True)]
  transfers between devices with their start and end apart: 2 -> 0, of which waited for: 2 -> 0; matrix products, arithmetic and copies ran while one was open for 0% -> 0% of each run, Pallas kernels for 0% -> 0%
where the time goes in v2:
time: 149 us; the launch traced here: 148 us
  Pallas kernels  147 us (99%)
    pallas_call x1, Pallas kernels, step(): pl.pallas_call(kernel, out_shape=pltpu.VMEM((R, D), BF), in_specs=[hbm] *...  147 us

profile of v2, /device:TPU:0, one launch (start us, length us, event | category | flops | bytes accessed | tf_op | source)
XLA Modules:
  0.0 148.2 jit_solution(16759089218967733674)
XLA Ops:
  0.0 146.7 %mlp.1 = bf16[192,6144]{1,0:T(8,128)(2,1)S(1)} custom-call(bf16[192,6144]{1,0:T(8,128)(2,1)} %x_hbm.1, bf16[6144,4096]{1,0:T(8,128)(2,1)} %wg.1, bf16[6144,4096]{1,0:T(8,128)(2,1)} %wu.1, bf16[4096,6144]{1,0:T(8,128)(2,1)} %wd.1), custom_call_target="tpu_custom_call" | custom-call | tf_op jit(solution)/shard_map/mlp/pallas_call | solution.py:297
  146.7 1.4 copy.6

commit v3 on v0

v3 whole, which is shorter than its diff:
```python
import jax
import jax.numpy as jnp
from jax import lax
from jax.experimental import pallas as pl
from jax.experimental.pallas import tpu as pltpu
from jax.sharding import PartitionSpec as P

D = 6144
F = 4096
R = 192
NB = 512
ND = D // NB
BF = jnp.bfloat16
F32 = jnp.float32
MESH = pl.DeviceIdType.MESH
PART = 1536
NP = D // PART

T_P = 5
T_MID = T_P + 6
T_FAR = T_MID + 3
T_OWN = T_FAR + ND
T_NEAR = T_OWN + 2
T_END = T_NEAR + ND // 2
RELAY = (3, T_P + 1, T_P + 3, T_MID)


def kernel(x_hbm, wg, wu, wd, out, X, H, W, S, rD, rR,
           wsem, lsem, ps, pr, xs, xr, ys, yr, ds_, dr, rs, rr, qs, qr):
    me = lax.axis_index("tp")
    partner = me + 1 - 2 * lax.rem(me, 2)
    remote = lax.rem(me + 2, 4)

    def rcopy(src, dst, s, r, dev):
        return pltpu.make_async_remote_copy(
            src_ref=src, dst_ref=dst, send_sem=s, recv_sem=r,
            device_id={"tp": dev}, device_id_type=MESH)

    def load_own():
        return pltpu.make_async_copy(x_hbm, X.at[pl.ds(0, R), :], lsem)

    def to_partner(c):
        rows = R // 2
        return rcopy(x_hbm.at[pl.ds(c * rows, rows), :], X.at[pl.ds(R + c * rows, rows), :],
                     ps.at[c], pr.at[c], partner)

    def to_remote(k):
        c = pl.ds(k * PART, PART)
        return rcopy(x_hbm.at[:, c], X.at[pl.ds(2 * R, R), c], xs.at[k], xr.at[k], remote)

    def relay(k):
        c = pl.ds(k * PART, PART)
        return rcopy(X.at[pl.ds(2 * R, R), c], X.at[pl.ds(3 * R, R), c], ys.at[k], yr.at[k], partner)

    def block(i):
        return pl.ds(pl.multiple_of(i * 512, 512), 512)

    def own_copies(i, slot):
        return [pltpu.make_async_copy(
            w.at[:, pl.ds(pl.multiple_of(i * 512 + b * 256, 256), 256)],
            W.at[slot, :, pl.ds(b * 512 + q * 256, 256)], wsem.at[slot, 2 * b + q])
            for b in range(2) for q, w in ((0, wg), (1, wu))]

    def part_copies(p, slot):
        rows = pl.ds(pl.multiple_of(p // 2 * PART, PART), PART)
        return [pltpu.make_async_copy(
            w.at[rows, block(p % 2 * 4 + e)],
            W.at[slot, pl.ds(e * PART, PART), pl.ds(q * 512, 512)], wsem.at[slot, 2 * e + q])
            for e in range(4) for q, w in ((0, wg), (1, wu))]

    def down_copy(pair, slot):
        c = pl.ds(pl.multiple_of(pair * 1024, 1024), 1024)
        return pltpu.make_async_copy(wd.at[:, c], W.at[slot, pl.ds(0, F), :], wsem.at[slot, 0])

    def own_block(t):
        return t - 6 * (t // T_MID) - (T_OWN - T_MID - 1) * (t // T_OWN) + 6 * (t // (2 * T_MID))

    def part_step(t):
        return t - T_P - t // (T_MID + 1)

    def cols(n):
        return pl.ds(pl.multiple_of(n * NB, NB), NB)

    def wide(n):
        return pl.ds(pl.multiple_of(n * 1024, 1024), 1024)

    def dot(a, w):
        return jnp.dot(a, w, preferred_element_type=F32)

    def own(rows, m, slot, i):
        for b in range(2):
            r = dot(X[pl.ds(rows, m), :], W[slot, :, pl.ds(b * 512, 512)])
            c = pl.ds(pl.multiple_of(i * 512 + b * 256, 256), 256)
            H[pl.ds(rows, m), c] = (jax.nn.silu(r[:, :256]) * r[:, 256:]).astype(BF)

    def part(slot, p, e, q):
        x = X[pl.ds(2 * R, 2 * R), pl.ds(pl.multiple_of(p // 2 * PART, PART), PART)]
        c = block((p % 2 * 4 + e) * 2 + q)
        return c, dot(x, W[slot, pl.ds(e * PART, PART), pl.ds(q * 512, 512)]) + S[:, c]

    load_own().start()
    for c in own_copies(0, 0):
        c.start()

    barrier = pltpu.get_barrier_semaphore()
    for dev in (partner, remote):
        pl.semaphore_signal(barrier, inc=1, device_id={"tp": dev}, device_id_type=MESH)
    pl.semaphore_wait(barrier, 2)
    to_remote(0).start()
    for c in range(2):
        to_partner(c).start()
    for k in range(1, NP):
        to_remote(k).start()
    for c in own_copies(1, 1):
        c.start()

    def clear(k, carry):
        S[pl.ds(pl.multiple_of(k * 8, 8), 8), :] = jnp.zeros((8, 2 * F), F32)
        return carry

    lax.fori_loop(0, 2 * R // 8, clear, 0)
    load_own().wait()
    for c in own_copies(0, 0):
        c.wait()
    own(0, R, 0, 0)
    for c in range(2):
        to_partner(c).wait_recv()
    own(R, R, 0, 0)

    def send_d(n):
        return rcopy(X.at[pl.ds(2 * R, R), cols(n)], rD.at[:, cols(n)], ds_.at[n], dr.at[n], partner)

    def send_r(n):
        return rcopy(X.at[pl.ds(3 * R, R), cols(n)], rR.at[:, cols(n)], rs.at[n], rr.at[n], remote)

    def landing(n):
        return pl.ds(pl.multiple_of(2 * R + lax.rem(n, 2) * R, 64), R)

    def send_p(n):
        return rcopy(X.at[pl.ds(0, R), wide(n)], H.at[landing(n), wide(n // 2)], qs.at[n], qr.at[n], partner)

    def held(n):
        return pl.ds(pl.multiple_of(lax.rem(n, 2) * NB, NB), NB)

    def prefetch_up(t):
        slot = lax.rem(t, 2)

        @pl.when((t < T_P) | (t == T_MID))
        def _():
            for c in own_copies(own_block(t), slot):
                c.start()

        @pl.when((t >= T_P) & (t < T_FAR) & (t != T_MID))
        def _():
            for c in part_copies(part_step(t), slot):
                c.start()

        @pl.when(t == T_FAR)
        def _():
            down_copy(0, slot).start()

    def wait_own(t, slot):
        for c in own_copies(own_block(t), slot):
            c.wait()

    def step(t, carry):
        slot = lax.rem(t, 2)

        @pl.when(t < T_FAR)
        def _():
            prefetch_up(t + 1)
            for k in range(NP):
                @pl.when(t == RELAY[k])
                def _(k=k):
                    to_remote(k).wait_recv()
                    relay(k).start()

            @pl.when((t >= T_P) & (t != T_MID))
            def _():
                p = part_step(t)
                for k in range(NP):
                    @pl.when(p == 2 * k)
                    def _(k=k):
                        relay(k).wait_recv()
                for c in part_copies(p, slot):
                    c.wait()

                @pl.when(t < T_MID)
                def _():
                    for e in range(4):
                        for q in range(2):
                            c, r = part(slot, p, e, q)
                            S[:, c] = r

                @pl.when(t > T_MID)
                def _():
                    for e in range(4):
                        c, r = part(slot, p, e, 0)
                        S[:, c] = jax.nn.silu(r)
                        up = part(slot, p, e, 1)[1]
                        H[pl.ds(2 * R, 2 * R), block(p % 2 * 4 + e)] = (S[:, c] * up).astype(BF)

        @pl.when((t >= T_FAR) & (t < T_NEAR))
        def _():
            n = t - T_FAR
            pair = n // 2

            @pl.when((lax.rem(n, 2) == 0) & (n < ND - 2))
            def _():
                down_copy(pair + 1, lax.rem(pair + 1, 2)).start()

            @pl.when((n == ND - 2) | (n == ND))
            def _():
                for c in own_copies(pair - ND // 2 + 7, lax.rem(pair + 1, 2)):
                    c.start()

            @pl.when(n == ND + 1)
            def _():
                down_copy(0, 0).start()

            @pl.when(n == 0)
            def _():
                for c in range(2):
                    to_partner(c).wait_send()
                for k in range(NP):
                    to_remote(k).wait_send()
                    relay(k).wait_send()

            @pl.when((n > 0) & (n <= ND))
            def _():
                send_d(n - 1).start()

            @pl.when(n > 1)
            def _():
                send_r(n - 2).start()

        @pl.when((t < T_P) | (t == T_MID) | ((t >= T_OWN) & (t < T_NEAR)))
        def _():
            wait_own(t, slot)
            own(0, 2 * R, slot, own_block(t))

        @pl.when((t >= T_FAR) & (t < T_OWN))
        def _():
            n = t - T_FAR
            s = lax.rem(n // 2, 2)

            @pl.when(lax.rem(n, 2) == 0)
            def _():
                down_copy(n // 2, s).wait()

            r = dot(H[pl.ds(2 * R, 2 * R), :], W[s, pl.ds(0, F), held(n)])
            S[pl.ds(R, R), held(n)] = r[:R]
            X[pl.ds(2 * R, R), cols(n)] = r[R:].astype(BF)

        @pl.when((t > T_FAR) & (t <= T_OWN))
        def _():
            n = t - T_FAR - 1
            send_d(n).wait_recv()
            X[pl.ds(3 * R, R), cols(n)] = (
                S[pl.ds(R, R), held(n)] + rD[:, cols(n)].astype(F32)).astype(BF)

        @pl.when(t >= T_NEAR)
        def _():
            m = t - T_NEAR

            @pl.when(m < ND // 2 - 1)
            def _():
                down_copy(m + 1, 1 - slot).start()

            @pl.when(m > 0)
            def _():
                send_p(m - 1).start()

            down_copy(m, slot).wait()
            for b in range(2):
                r = dot(H[pl.ds(0, 2 * R), :], W[slot, pl.ds(0, F), pl.ds(b * NB, NB)])
                c = cols(2 * m + b)
                S[pl.ds(0, R), c] = r[:R]
                X[pl.ds(0, R), c] = r[R:].astype(BF)

        return carry

    lax.fori_loop(1, T_END, step, 0)
    send_p(ND // 2 - 1).start()

    def finish(n, carry):
        @pl.when(lax.rem(n, 2) == 0)
        def _():
            send_p(n // 2).wait_recv()
        send_r(n).wait_recv()
        near = H[landing(n // 2), cols(n // 4 * 2 + lax.rem(n, 2))]
        out[:, cols(n)] = (S[pl.ds(0, R), cols(n)] + near.astype(F32)
                           + rR[:, cols(n)].astype(F32)).astype(BF)
        return carry

    lax.fori_loop(0, ND, finish, 0)

    def drain(n, carry):
        send_d(n).wait_send()
        send_r(n).wait_send()
        return carry

    lax.fori_loop(0, ND, drain, 0)
    for n in range(ND // 2):
        send_p(n).wait_send()


def solution(mesh):
    dma = pltpu.SemaphoreType.DMA

    def step(x, w_gate, w_up, w_down):
        hbm = pl.BlockSpec(memory_space=pl.ANY)
        return pl.pallas_call(
            kernel,
            out_shape=pltpu.VMEM((R, D), BF),
            in_specs=[hbm] * 4,
            out_specs=pl.BlockSpec(memory_space=pltpu.VMEM),
            scratch_shapes=[
                pltpu.VMEM((4 * R, D), BF),
                pltpu.VMEM((4 * R, F), BF),
                pltpu.VMEM((2, D, 1024), BF),
                pltpu.VMEM((2 * R, 2 * F), F32),
                pltpu.VMEM((R, D), BF),
                pltpu.VMEM((R, D), BF),
                dma((2, 8)), dma,
                dma((2,)), dma((2,)),
                dma((NP,)), dma((NP,)),
                dma((NP,)), dma((NP,)),
                dma((ND,)), dma((ND,)),
                dma((ND,)), dma((ND,)),
                dma((ND // 2,)), dma((ND // 2,)),
            ],
            compiler_params=pltpu.CompilerParams(
                collective_id=0, has_side_effects=True, vmem_limit_bytes=64500000),
            name="mlp",
        )(x, w_gate, w_up, w_down)

    return jax.shard_map(
        step,
        mesh=mesh,
        in_specs=(P(("dp", "tp"), None), P(None, "tp"), P(None, "tp"), P("tp", None)),
        out_specs=P(("dp", "tp"), None),
        check_vma=False,
    )
```

time: 294 us -> 140 us (0.48)
  matrix products: 142 us -> 0 us
  waiting for transfers between devices: 139 us -> 0 us
  Pallas kernels: 0 us -> 138 us
  between operations: 13.4 us -> 0.01 us
    dot_general x3 -> x0, matrix products: 142 us -> none  [the longest x1 51.8 us: step(): gate = jnp.dot(rows, w_gate, preferred_element_type=jnp.float32)]
    pallas_call x0 -> x1, Pallas kernels: none -> 138 us  [step(): pl.pallas_call(kernel, out_shape=pltpu.VMEM((R, D), BF), in_specs=[hbm] *...]
    reduce_scatter x1 -> x0, waiting for transfers between devices: 71.7 us -> none  [step(): return lax.psum_scatter(term, 'tp', scatter_dimension=0, tiled=True)]
    all_gather x1 -> x0, waiting for transfers between devices: 66.2 us -> none  [step(): rows = lax.all_gather(x, 'tp', axis=0, tiled=True)]
  transfers between devices with their start and end apart: 2 -> 0, of which waited for: 2 -> 0; matrix products, arithmetic and copies ran while one was open for 0% -> 0% of each run, Pallas kernels for 0% -> 0%
where the time goes in v3:
time: 140 us
  Pallas kernels  138 us (99%)
  local copies, waits for them, and re-layouts  1.41 us (1%)
    pallas_call x1, Pallas kernels, step(): pl.pallas_call(kernel, out_shape=pltpu.VMEM((R, D), BF), in_specs=[hbm] *...  138 us

profile of v3, /device:TPU:0, one launch (start us, length us, event | category | flops | bytes accessed | tf_op | source)
XLA Modules:
  0.0 139.7 jit_solution(12150616263217229539)
XLA Ops:
  0.0 138.3 %mlp.1 = bf16[192,6144]{1,0:T(8,128)(2,1)S(1)} custom-call(bf16[192,6144]{1,0:T(8,128)(2,1)} %x_hbm.1, bf16[6144,4096]{1,0:T(8,128)(2,1)} %wg.1, bf16[6144,4096]{1,0:T(8,128)(2,1)} %wu.1, bf16[4096,6144]{1,0:T(8,128)(2,1)} %wd.1), custom_call_target="tpu_custom_call" | custom-call | tf_op jit(solution)/shard_map/mlp/pallas_call | solution.py:313
  138.3 1.4 %copy.6 = bf16[192,6144]{1,0:T(8,128)(2,1)} copy(bf16[192,6144]{1,0:T(8,128)(2,1)S(1)} %mlp.1) | data formatting | bytes 4718592

commit v4 on v3

v4 whole, which is shorter than its diff:
```python
import jax
import jax.numpy as jnp
from jax import lax
from jax.experimental import pallas as pl
from jax.experimental.pallas import tpu as pltpu
from jax.sharding import PartitionSpec as P

D = 6144
F = 4096
R = 192
NB = 512
ND = D // NB
BF = jnp.bfloat16
F32 = jnp.float32
MESH = pl.DeviceIdType.MESH
PART = 1536
NP = D // PART

T_P = 5
T_FAR = T_P + 2 * NP
T_OWN = T_FAR + ND // 2 + 1
T_NEAR = T_OWN + 3
T_END = T_NEAR + ND // 2
RELAY = (3, T_P + 1, T_P + 3, T_P + 5)
NU = ND // 2 + 1


def kernel(x_hbm, wg, wu, wd, out, X, H, W, S, rD, rR,
           wsem, lsem, ps, pr, xs, xr, ys, yr, ds_, dr, rs, rr, qs, qr):
    me = lax.axis_index("tp")
    partner = me + 1 - 2 * lax.rem(me, 2)
    remote = lax.rem(me + 2, 4)

    def rcopy(src, dst, s, r, dev):
        return pltpu.make_async_remote_copy(
            src_ref=src, dst_ref=dst, send_sem=s, recv_sem=r,
            device_id={"tp": dev}, device_id_type=MESH)

    def load_own():
        return pltpu.make_async_copy(x_hbm, X.at[pl.ds(0, R), :], lsem)

    def to_partner(c):
        rows = R // 2
        return rcopy(x_hbm.at[pl.ds(c * rows, rows), :], X.at[pl.ds(R + c * rows, rows), :],
                     ps.at[c], pr.at[c], partner)

    def to_remote(k):
        c = pl.ds(k * PART, PART)
        return rcopy(x_hbm.at[:, c], X.at[pl.ds(2 * R, R), c], xs.at[k], xr.at[k], remote)

    def relay(k):
        c = pl.ds(k * PART, PART)
        return rcopy(X.at[pl.ds(2 * R, R), c], X.at[pl.ds(3 * R, R), c], ys.at[k], yr.at[k], partner)

    def block(i):
        return pl.ds(pl.multiple_of(i * 512, 512), 512)

    def own_copies(i, slot, halves=(0, 1)):
        return [pltpu.make_async_copy(
            w.at[:, pl.ds(pl.multiple_of(i * 512 + b * 256, 256), 256)],
            W.at[slot, :, pl.ds(b * 512 + q * 256, 256)], wsem.at[slot, 2 * b + q])
            for b in halves for q, w in ((0, wg), (1, wu))]

    def part_copies(p, slot):
        rows = pl.ds(pl.multiple_of(p // 2 * PART, PART), PART)
        return [pltpu.make_async_copy(
            w.at[rows, block(p % 2 * 4 + e)],
            W.at[slot, pl.ds(e * PART, PART), pl.ds(q * 512, 512)], wsem.at[slot, 2 * e + q])
            for e in range(4) for q, w in ((0, wg), (1, wu))]

    def down_copy(pair, slot):
        c = pl.ds(pl.multiple_of(pair * 1024, 1024), 1024)
        return pltpu.make_async_copy(wd.at[:, c], W.at[slot, pl.ds(0, F), :], wsem.at[slot, 0])

    def own_block(t):
        return t - (T_OWN - T_P) * (t // T_OWN)

    def cols(n):
        return pl.ds(pl.multiple_of(n * NB, NB), NB)

    def wide(n):
        return pl.ds(pl.multiple_of(n * 1024, 1024), 1024)

    def dot(a, w):
        return jnp.dot(a, w, preferred_element_type=F32)

    def own(rows, m, slot, i, halves=(0, 1)):
        for b in halves:
            r = dot(X[pl.ds(rows, m), :], W[slot, :, pl.ds(b * 512, 512)])
            c = pl.ds(pl.multiple_of(i * 512 + b * 256, 256), 256)
            H[pl.ds(rows, m), c] = (jax.nn.silu(r[:, :256]) * r[:, 256:]).astype(BF)

    def part(slot, p, e, q):
        x = X[pl.ds(2 * R, 2 * R), pl.ds(pl.multiple_of(p // 2 * PART, PART), PART)]
        c = block((p % 2 * 4 + e) * 2 + q)
        return c, dot(x, W[slot, pl.ds(e * PART, PART), pl.ds(q * 512, 512)]) + S[:, c]

    load_own().start()
    for c in own_copies(0, 0, (0,)):
        c.start()

    barrier = pltpu.get_barrier_semaphore()
    for dev in (partner, remote):
        pl.semaphore_signal(barrier, inc=1, device_id={"tp": dev}, device_id_type=MESH)

    def clear(k, carry):
        S[pl.ds(pl.multiple_of(k * 8, 8), 8), :] = jnp.zeros((8, 2 * F), F32)
        return carry

    lax.fori_loop(0, 2 * R // 8, clear, 0)
    pl.semaphore_wait(barrier, 2)
    to_remote(0).start()
    for c in range(2):
        to_partner(c).start()
    for k in range(1, NP):
        to_remote(k).start()
    for c in own_copies(0, 0, (1,)) + own_copies(1, 1):
        c.start()
    load_own().wait()
    for b in range(2):
        for c in own_copies(0, 0, (b,)):
            c.wait()
        own(0, R, 0, 0, (b,))
    for c in range(2):
        to_partner(c).wait_recv()
    own(R, R, 0, 0)

    def far_copy(u, rows, dst, s, r, dev, go):
        @pl.when(u < 2)
        def _():
            c = cols(u)
            go(rcopy(X.at[rows, c], dst.at[:, c], s.at[u], r.at[u], dev))

        @pl.when(u >= 2)
        def _():
            c = wide(u - 1)
            go(rcopy(X.at[rows, c], dst.at[:, c], s.at[u], r.at[u], dev))

    def send_d(u, go):
        far_copy(u, pl.ds(2 * R, R), rD, ds_, dr, partner, go)

    def send_r(u, go):
        far_copy(u, pl.ds(3 * R, R), rR, rs, rr, remote, go)

    start = lambda c: c.start()
    wait_send = lambda c: c.wait_send()
    wait_recv = lambda c: c.wait_recv()

    def landing(n):
        return pl.ds(pl.multiple_of(2 * R + lax.rem(n, 2) * R, 64), R)

    def send_p(n):
        return rcopy(X.at[pl.ds(0, R), wide(n)], H.at[landing(n), wide(n // 2)], qs.at[n], qr.at[n], partner)

    def pair_sum(c, h):
        X[pl.ds(3 * R, R), c] = (S[pl.ds(R, R), h] + rD[:, c].astype(F32)).astype(BF)

    def down(rows, slot, w, keep_rows, keep, send_rows, c):
        r = dot(H[pl.ds(rows, 2 * R), :], W[slot, pl.ds(0, F), w])
        S[keep_rows, keep] = r[:R]
        X[send_rows, c] = r[R:].astype(BF)

    def step(t, carry):
        late = t // (T_FAR + 1) - t // (2 * T_FAR + 2)
        slot = lax.rem(t + late, 2)
        other = 1 - slot

        @pl.when(t < T_FAR)
        def _():
            @pl.when(t < T_P - 1)
            def _():
                for c in own_copies(t + 1, other):
                    c.start()

            @pl.when((t >= T_P - 1) & (t < T_FAR - 1))
            def _():
                for c in part_copies(t + 1 - T_P, other):
                    c.start()

            @pl.when(t == T_FAR - 1)
            def _():
                down_copy(0, other).start()

            @pl.when((t == RELAY[0]) | (t == RELAY[1]) | (t == RELAY[2]) | (t == RELAY[3]))
            def _():
                for k in range(NP):
                    @pl.when(t == RELAY[k])
                    def _(k=k):
                        to_remote(k).wait_recv()
                        relay(k).start()

            @pl.when(t >= T_P)
            def _():
                p = t - T_P

                @pl.when(lax.rem(p, 2) == 0)
                def _():
                    for k in range(NP):
                        @pl.when(p == 2 * k)
                        def _(k=k):
                            relay(k).wait_recv()

                for c in part_copies(p, slot):
                    c.wait()

                @pl.when(p < 2 * NP - 2)
                def _():
                    for e in range(4):
                        for q in range(2):
                            c, r = part(slot, p, e, q)
                            S[:, c] = r

                @pl.when(p >= 2 * NP - 2)
                def _():
                    for e in range(4):
                        c, r = part(slot, p, e, 0)
                        S[:, c] = jax.nn.silu(r)
                        up = part(slot, p, e, 1)[1]
                        H[pl.ds(2 * R, 2 * R), block(lax.rem(p, 2) * 4 + e)] = (S[:, c] * up).astype(BF)

        @pl.when((t >= T_FAR) & (t < T_NEAR))
        def _():
            u = t - T_FAR

            @pl.when(u == 0)
            def _():
                down_copy(1, other).start()
                for c in range(2):
                    to_partner(c).wait_send()
                for k in range(NP):
                    to_remote(k).wait_send()
                    relay(k).wait_send()

            @pl.when((u > 1) & (u < NU - 1))
            def _():
                down_copy(u, other).start()

            @pl.when((u >= NU - 1) & (u < NU + 2))
            def _():
                for c in own_copies(T_P + u - NU + 1, other):
                    c.start()

            @pl.when(u == NU + 2)
            def _():
                down_copy(0, other).start()

            @pl.when((u > 0) & (u <= NU))
            def _():
                send_d(u - 1, start)

            @pl.when((u > 1) & (u <= NU + 1))
            def _():
                send_r(u - 2, start)

            @pl.when(u < 2)
            def _():
                @pl.when(u == 0)
                def _():
                    down_copy(0, T_FAR % 2).wait()

                down(2 * R, T_FAR % 2, cols(u), pl.ds(R, R), cols(u), pl.ds(2 * R, R), cols(u))

        @pl.when((t < T_P) | ((t >= T_OWN) & (t < T_NEAR)))
        def _():
            i = own_block(t)
            for c in own_copies(i, slot):
                c.wait()
            own(0, 2 * R, slot, i)

        @pl.when(((t >= T_FAR + 2) & (t < T_OWN)) | (t >= T_NEAR))
        def _():
            near = t // T_NEAR
            m = t - T_FAR - 1 - (T_NEAR - T_FAR - 1) * near

            @pl.when((t >= T_NEAR) & (m < ND // 2 - 1))
            def _():
                down_copy(m + 1, other).start()

            @pl.when((t >= T_NEAR) & (m > 0))
            def _():
                send_p(m - 1).start()

            down_copy(m, slot).wait()
            far = 1 - near
            k = 2 * (lax.rem(m, 2) * far + m * near)
            for b in range(2):
                down(pl.multiple_of(2 * R * far, 128), slot, pl.ds(b * NB, NB),
                     pl.ds(pl.multiple_of(R * far, 64), R), cols(k + b),
                     pl.ds(pl.multiple_of(2 * R * far, 128), R), cols(2 * m + b))

        @pl.when((t > T_FAR) & (t <= T_OWN))
        def _():
            u = t - T_FAR - 1
            send_d(u, wait_recv)

            @pl.when(u < 2)
            def _():
                pair_sum(cols(u), cols(u))

            @pl.when(u >= 2)
            def _():
                pair_sum(wide(u - 1), wide(lax.rem(u - 1, 2)))

        return carry

    lax.fori_loop(1, T_END, step, 0)
    send_p(ND // 2 - 1).start()

    def finish(n, carry):
        send_p(n).wait_recv()

        @pl.when(n == 0)
        def _():
            send_r(0, wait_recv)

        send_r(n + 1, wait_recv)
        out[:, wide(n)] = (S[pl.ds(0, R), wide(n)] + H[landing(n), wide(n // 2)].astype(F32)
                           + rR[:, wide(n)].astype(F32)).astype(BF)
        return carry

    lax.fori_loop(0, ND // 2, finish, 0)

    def drain(u, carry):
        send_d(u, wait_send)
        send_r(u, wait_send)
        return carry

    lax.fori_loop(0, NU, drain, 0)
    for n in range(ND // 2):
        send_p(n).wait_send()


def solution(mesh):
    dma = pltpu.SemaphoreType.DMA

    def step(x, w_gate, w_up, w_down):
        hbm = pl.BlockSpec(memory_space=pl.ANY)
        return pl.pallas_call(
            kernel,
            out_shape=pltpu.VMEM((R, D), BF),
            in_specs=[hbm] * 4,
            out_specs=pl.BlockSpec(memory_space=pltpu.VMEM),
            scratch_shapes=[
                pltpu.VMEM((4 * R, D), BF),
                pltpu.VMEM((4 * R, F), BF),
                pltpu.VMEM((2, D, 1024), BF),
                pltpu.VMEM((2 * R, 2 * F), F32),
                pltpu.VMEM((R, D), BF),
                pltpu.VMEM((R, D), BF),
                dma((2, 8)), dma,
                dma((2,)), dma((2,)),
                dma((NP,)), dma((NP,)),
                dma((NP,)), dma((NP,)),
                dma((NU,)), dma((NU,)),
                dma((NU,)), dma((NU,)),
                dma((ND // 2,)), dma((ND // 2,)),
            ],
            compiler_params=pltpu.CompilerParams(
                collective_id=0, has_side_effects=True, vmem_limit_bytes=64500000),
            name="mlp",
        )(x, w_gate, w_up, w_down)

    return jax.shard_map(
        step,
        mesh=mesh,
        in_specs=(P(("dp", "tp"), None), P(None, "tp"), P(None, "tp"), P("tp", None)),
        out_specs=P(("dp", "tp"), None),
        check_vma=False,
    )
```

time: 140 us -> 136 us (0.971)
  Pallas kernels: 138 us -> 135 us
    pallas_call x1, Pallas kernels: 138 us -> 135 us  [step(): pl.pallas_call(kernel, out_shape=pltpu.VMEM((R, D), BF), in_specs=[hbm] *...]
where the time goes in v4:
time: 136 us
  Pallas kernels  135 us (99%)
  local copies, waits for them, and re-layouts  1.41 us (1%)
    pallas_call x1, Pallas kernels, step(): pl.pallas_call(kernel, out_shape=pltpu.VMEM((R, D), BF), in_specs=[hbm] *...  135 us

profile of v4, /device:TPU:0, one launch (start us, length us, event | category | flops | bytes accessed | tf_op | source)
XLA Modules:
  0.0 136.0 jit_solution(8306305951821437205)
XLA Ops:
  0.0 134.6 %mlp.1 = bf16[192,6144]{1,0:T(8,128)(2,1)S(1)} custom-call(bf16[192,6144]{1,0:T(8,128)(2,1)} %x_hbm.1, bf16[6144,4096]{1,0:T(8,128)(2,1)} %wg.1, bf16[6144,4096]{1,0:T(8,128)(2,1)} %wu.1, bf16[4096,6144]{1,0:T(8,128)(2,1)} %wd.1), custom_call_target="tpu_custom_call" | custom-call | tf_op jit(solution)/shard_map/mlp/pallas_call | solution.py:338
  134.6 1.4 %copy.6 = bf16[192,6144]{1,0:T(8,128)(2,1)} copy(bf16[192,6144]{1,0:T(8,128)(2,1)S(1)} %mlp.1) | data formatting | bytes 4718592

commit v5 on v4

--- a/solution.py
+++ b/solution.py
@@ -20,7 +20,7 @@
 T_FAR = T_P + 2 * NP
 T_OWN = T_FAR + ND // 2 + 1
 T_NEAR = T_OWN + 3
-T_END = T_NEAR + ND // 2
+T_END = T_NEAR + ND // 2 - 1
 RELAY = (3, T_P + 1, T_P + 3, T_P + 5)
 NU = ND // 2 + 1
 
@@ -55,10 +55,10 @@
     def block(i):
         return pl.ds(pl.multiple_of(i * 512, 512), 512)
 
-    def own_copies(i, slot, halves=(0, 1)):
+    def own_copies(i, slot, halves=(0, 1), rows=pl.ds(0, D)):
         return [pltpu.make_async_copy(
-            w.at[:, pl.ds(pl.multiple_of(i * 512 + b * 256, 256), 256)],
-            W.at[slot, :, pl.ds(b * 512 + q * 256, 256)], wsem.at[slot, 2 * b + q])
+            w.at[rows, pl.ds(pl.multiple_of(i * 512 + b * 256, 256), 256)],
+            W.at[slot, rows, pl.ds(b * 512 + q * 256, 256)], wsem.at[slot, 2 * b + q])
             for b in halves for q, w in ((0, wg), (1, wu))]
 
     def part_copies(p, slot):
@@ -70,16 +70,19 @@
 
     def down_copy(pair, slot):
         c = pl.ds(pl.multiple_of(pair * 1024, 1024), 1024)
-        return pltpu.make_async_copy(wd.at[:, c], W.at[slot, pl.ds(0, F), :], wsem.at[slot, 0])
+        return pltpu.make_async_copy(wd.at[:, c], W.at[slot, pl.ds(0, F), :], wsem.at[slot, 7])
 
     def own_block(t):
         return t - (T_OWN - T_P) * (t // T_OWN)
 
+    def at(start, size):
+        return pl.ds(start if isinstance(start, int) else pl.multiple_of(start, size), size)
+
     def cols(n):
-        return pl.ds(pl.multiple_of(n * NB, NB), NB)
+        return at(n * NB, NB)
 
     def wide(n):
-        return pl.ds(pl.multiple_of(n * 1024, 1024), 1024)
+        return at(n * 1024, 1024)
 
     def dot(a, w):
         return jnp.dot(a, w, preferred_element_type=F32)
@@ -108,13 +111,15 @@
         return carry
 
     lax.fori_loop(0, 2 * R // 8, clear, 0)
+    for c in own_copies(0, 0, (1,)):
+        c.start()
     pl.semaphore_wait(barrier, 2)
     to_remote(0).start()
     for c in range(2):
         to_partner(c).start()
     for k in range(1, NP):
         to_remote(k).start()
-    for c in own_copies(0, 0, (1,)) + own_copies(1, 1):
+    for c in own_copies(1, 1):
         c.start()
     load_own().wait()
     for b in range(2):
@@ -126,6 +131,11 @@
     own(R, R, 0, 0)
 
     def far_copy(u, rows, dst, s, r, dev, go):
+        if isinstance(u, int):
+            c = cols(u) if u < 2 else wide(u - 1)
+            go(rcopy(X.at[rows, c], dst.at[:, c], s.at[u], r.at[u], dev))
+            return
+
         @pl.when(u < 2)
         def _():
             c = cols(u)
@@ -147,7 +157,7 @@
     wait_recv = lambda c: c.wait_recv()
 
     def landing(n):
-        return pl.ds(pl.multiple_of(2 * R + lax.rem(n, 2) * R, 64), R)
+        return pl.ds(2 * R + n % 2 * R, R)
 
     def send_p(n):
         return rcopy(X.at[pl.ds(0, R), wide(n)], H.at[landing(n), wide(n // 2)], qs.at[n], qr.at[n], partner)
@@ -235,7 +245,17 @@
             def _():
                 down_copy(u, other).start()
 
-            @pl.when((u >= NU - 1) & (u < NU + 2))
+            @pl.when(u == NU - 2)
+            def _():
+                for c in own_copies(T_P, slot, rows=pl.ds(F, D - F)):
+                    c.start()
+
+            @pl.when(u == NU - 1)
+            def _():
+                for c in own_copies(T_P, other, rows=pl.ds(0, F)):
+                    c.start()
+
+            @pl.when((u >= NU) & (u < NU + 2))
             def _():
                 for c in own_copies(T_P + u - NU + 1, other):
                     c.start()
@@ -272,7 +292,7 @@
             near = t // T_NEAR
             m = t - T_FAR - 1 - (T_NEAR - T_FAR - 1) * near
 
-            @pl.when((t >= T_NEAR) & (m < ND // 2 - 1))
+            @pl.when(t >= T_NEAR)
             def _():
                 down_copy(m + 1, other).start()
 
@@ -304,21 +324,32 @@
         return carry
 
     lax.fori_loop(1, T_END, step, 0)
-    send_p(ND // 2 - 1).start()
-
-    def finish(n, carry):
+
+    last = ND // 2 - 1
+
+    def arrived(n):
         send_p(n).wait_recv()
-
-        @pl.when(n == 0)
-        def _():
+        if n == 0:
             send_r(0, wait_recv)
-
         send_r(n + 1, wait_recv)
+
+    def finish(n):
         out[:, wide(n)] = (S[pl.ds(0, R), wide(n)] + H[landing(n), wide(n // 2)].astype(F32)
                            + rR[:, wide(n)].astype(F32)).astype(BF)
-        return carry
-
-    lax.fori_loop(0, ND // 2, finish, 0)
+
+    def last_dot(rows, b):
+        return dot(H[pl.ds(rows, R), :], W[(T_END + 1) % 2, pl.ds(0, F), pl.ds(b * NB, NB)])
+
+    send_p(last - 1).start()
+    down_copy(last, (T_END + 1) % 2).wait()
+    for b in range(2):
+        X[pl.ds(0, R), cols(2 * last + b)] = last_dot(R, b).astype(BF)
+    send_p(last).start()
+    for b in range(2):
+        S[pl.ds(0, R), cols(2 * last + b)] = last_dot(0, b)
+    for n in range(last + 1):
+        arrived(n)
+        finish(n)
 
     def drain(u, carry):
         send_d(u, wait_send)

time: 136 us -> 134 us (0.985)
  Pallas kernels: 135 us -> 133 us
    pallas_call x1, Pallas kernels: 135 us -> 133 us  [step(): pl.pallas_call(kernel, out_shape=pltpu.VMEM((R, D), BF), in_specs=[hbm] *...]
where the time goes in v5:
time: 134 us
  Pallas kernels  133 us (99%)
  local copies, waits for them, and re-layouts  1.41 us (1%)
    pallas_call x1, Pallas kernels, step(): pl.pallas_call(kernel, out_shape=pltpu.VMEM((R, D), BF), in_specs=[hbm] *...  133 us

profile of v5, /device:TPU:0, one launch (start us, length us, event | category | flops | bytes accessed | tf_op | source)
XLA Modules:
  0.0 134.0 jit_solution(1384165497047341459)
XLA Ops:
  0.0 132.6 %mlp.1 = bf16[192,6144]{1,0:T(8,128)(2,1)S(1)} custom-call(bf16[192,6144]{1,0:T(8,128)(2,1)} %x_hbm.1, bf16[6144,4096]{1,0:T(8,128)(2,1)} %wg.1, bf16[6144,4096]{1,0:T(8,128)(2,1)} %wu.1, bf16[4096,6144]{1,0:T(8,128)(2,1)} %wd.1), custom_call_target="tpu_custom_call" | custom-call | tf_op jit(solution)/shard_map/mlp/pallas_call | solution.py:369
  132.6 1.4 %copy.6 = bf16[192,6144]{1,0:T(8,128)(2,1)} copy(bf16[192,6144]{1,0:T(8,128)(2,1)S(1)} %mlp.1) | data formatting | bytes 4718592

commit v6 on v5

--- a/solution.py
+++ b/solution.py
@@ -25,7 +25,7 @@
 NU = ND // 2 + 1
 
 
-def kernel(x_hbm, wg, wu, wd, out, X, H, W, S, rD, rR,
+def kernel(x_hbm, wg, wu, wd, out, X, H, W, S, T, rD, rR,
            wsem, lsem, ps, pr, xs, xr, ys, yr, ds_, dr, rs, rr, qs, qr):
     me = lax.axis_index("tp")
     partner = me + 1 - 2 * lax.rem(me, 2)
@@ -98,9 +98,27 @@
         c = block((p % 2 * 4 + e) * 2 + q)
         return c, dot(x, W[slot, pl.ds(e * PART, PART), pl.ds(q * 512, 512)]) + S[:, c]
 
+    KH = D // 2
+
+    def quarter(b, k):
+        rows = pl.ds(k * KH, KH)
+        return [pltpu.make_async_copy(
+            w.at[rows, pl.ds(b * 256, 256)],
+            W.at[0, rows, pl.ds(b * 512 + q * 256, 256)], wsem.at[0, 4 * k + 2 * b + q])
+            for q, w in ((0, wg), (1, wu))]
+
+    def start_quarter(b, k):
+        for c in quarter(b, k):
+            c.start()
+
+    def quarter_dot(b, k):
+        for c in quarter(b, k):
+            c.wait()
+        rows = pl.ds(k * KH, KH)
+        return dot(X[pl.ds(0, R), rows], W[0, rows, pl.ds(b * 512, 512)])
+
     load_own().start()
-    for c in own_copies(0, 0, (0,)):
-        c.start()
+    start_quarter(0, 0)
 
     barrier = pltpu.get_barrier_semaphore()
     for dev in (partner, remote):
@@ -110,22 +128,23 @@
         S[pl.ds(pl.multiple_of(k * 8, 8), 8), :] = jnp.zeros((8, 2 * F), F32)
         return carry
 
-    lax.fori_loop(0, 2 * R // 8, clear, 0)
-    for c in own_copies(0, 0, (1,)):
-        c.start()
+    lax.fori_loop(0, R // 8, clear, 0)
+    start_quarter(0, 1)
+    lax.fori_loop(R // 8, 2 * R // 8, clear, 0)
+    start_quarter(1, 0)
+    start_quarter(1, 1)
     pl.semaphore_wait(barrier, 2)
-    to_remote(0).start()
     for c in range(2):
         to_partner(c).start()
-    for k in range(1, NP):
+    for k in range(NP):
         to_remote(k).start()
     for c in own_copies(1, 1):
         c.start()
     load_own().wait()
     for b in range(2):
-        for c in own_copies(0, 0, (b,)):
-            c.wait()
-        own(0, R, 0, 0, (b,))
+        T[...] = quarter_dot(b, 0)
+        r = quarter_dot(b, 1) + T[...]
+        H[pl.ds(0, R), pl.ds(b * 256, 256)] = (jax.nn.silu(r[:, :256]) * r[:, 256:]).astype(BF)
     for c in range(2):
         to_partner(c).wait_recv()
     own(R, R, 0, 0)
@@ -340,6 +359,11 @@
     def last_dot(rows, b):
         return dot(H[pl.ds(rows, R), :], W[(T_END + 1) % 2, pl.ds(0, F), pl.ds(b * NB, NB)])
 
+    def drain(u, carry):
+        send_d(u, wait_send)
+        send_r(u, wait_send)
+        return carry
+
     send_p(last - 1).start()
     down_copy(last, (T_END + 1) % 2).wait()
     for b in range(2):
@@ -347,17 +371,14 @@
     send_p(last).start()
     for b in range(2):
         S[pl.ds(0, R), cols(2 * last + b)] = last_dot(0, b)
-    for n in range(last + 1):
+    for n in range(last):
         arrived(n)
         finish(n)
-
-    def drain(u, carry):
-        send_d(u, wait_send)
-        send_r(u, wait_send)
-        return carry
-
-    lax.fori_loop(0, NU, drain, 0)
-    for n in range(ND // 2):
+    lax.fori_loop(0, NU - 1, drain, 0)
+    arrived(last)
+    finish(last)
+    drain(NU - 1, 0)
+    for n in range(last + 1):
         send_p(n).wait_send()
 
 
@@ -376,6 +397,7 @@
                 pltpu.VMEM((4 * R, F), BF),
                 pltpu.VMEM((2, D, 1024), BF),
                 pltpu.VMEM((2 * R, 2 * F), F32),
+                pltpu.VMEM((R, NB), F32),
                 pltpu.VMEM((R, D), BF),
                 pltpu.VMEM((R, D), BF),
                 dma((2, 8)), dma,

time: 134 us -> 134 us (level)
  no operation moved by 1% of the time
where the time goes in v6:
time: 134 us
  Pallas kernels  133 us (99%)
  local copies, waits for them, and re-layouts  1.41 us (1%)
    pallas_call x1, Pallas kernels, step(): pl.pallas_call(kernel, out_shape=pltpu.VMEM((R, D), BF), in_specs=[hbm] *...  133 us

profile of v6, /device:TPU:0, one launch (start us, length us, event | category | flops | bytes accessed | tf_op | source)
XLA Modules:
  0.0 133.9 jit_solution(10024364591997013505)
XLA Ops:
  0.0 132.5 %mlp.1 = bf16[192,6144]{1,0:T(8,128)(2,1)S(1)} custom-call(bf16[192,6144]{1,0:T(8,128)(2,1)} %x_hbm.1, bf16[6144,4096]{1,0:T(8,128)(2,1)} %wg.1, bf16[6144,4096]{1,0:T(8,128)(2,1)} %wu.1, bf16[4096,6144]{1,0:T(8,128)(2,1)} %wd.1), custom_call_target="tpu_custom_call" | custom-call | tf_op jit(solution)/shard_map/mlp/pallas_call | solution.py:390
  132.5 1.4 %copy.6 = bf16[192,6144]{1,0:T(8,128)(2,1)} copy(bf16[192,6144]{1,0:T(8,128)(2,1)S(1)} %mlp.1) | data formatting | bytes 4718592

commit v7 on v6

--- a/solution.py
+++ b/solution.py
@@ -16,13 +16,14 @@
 PART = 1536
 NP = D // PART
 
+NT = ND // 3
+NU = 3 + NT - 1
 T_P = 5
 T_FAR = T_P + 2 * NP
-T_OWN = T_FAR + ND // 2 + 1
+T_OWN = T_FAR + NU
 T_NEAR = T_OWN + 3
-T_END = T_NEAR + ND // 2 - 1
+T_END = T_NEAR + NT - 1
 RELAY = (3, T_P + 1, T_P + 3, T_P + 5)
-NU = ND // 2 + 1
 
 
 def kernel(x_hbm, wg, wu, wd, out, X, H, W, S, T, rD, rR,
@@ -55,11 +56,11 @@
     def block(i):
         return pl.ds(pl.multiple_of(i * 512, 512), 512)
 
-    def own_copies(i, slot, halves=(0, 1), rows=pl.ds(0, D)):
+    def own_copies(i, slot):
         return [pltpu.make_async_copy(
-            w.at[rows, pl.ds(pl.multiple_of(i * 512 + b * 256, 256), 256)],
-            W.at[slot, rows, pl.ds(b * 512 + q * 256, 256)], wsem.at[slot, 2 * b + q])
-            for b in halves for q, w in ((0, wg), (1, wu))]
+            w.at[:, pl.ds(pl.multiple_of(i * 512 + b * 256, 256), 256)],
+            W.at[slot, :, pl.ds(b * 512 + q * 256, 256)], wsem.at[slot, 2 * b + q])
+            for b in range(2) for q, w in ((0, wg), (1, wu))]
 
     def part_copies(p, slot):
         rows = pl.ds(pl.multiple_of(p // 2 * PART, PART), PART)
@@ -68,9 +69,22 @@
             W.at[slot, pl.ds(e * PART, PART), pl.ds(q * 512, 512)], wsem.at[slot, 2 * e + q])
             for e in range(4) for q, w in ((0, wg), (1, wu))]
 
-    def down_copy(pair, slot):
-        c = pl.ds(pl.multiple_of(pair * 1024, 1024), 1024)
-        return pltpu.make_async_copy(wd.at[:, c], W.at[slot, pl.ds(0, F), :], wsem.at[slot, 7])
+    def down_copies(g, slot):
+        two = pl.ds(pl.multiple_of(g * 3 * NB, NB), 2 * NB)
+        third = pl.ds(pl.multiple_of(g * 3 * NB + 2 * NB, NB), NB)
+        return [pltpu.make_async_copy(wd.at[:, two], W.at[slot, pl.ds(0, F), :], wsem.at[slot, 5])] + [
+            pltpu.make_async_copy(
+                wd.at[pl.ds(k * F // 2, F // 2), third],
+                W.at[slot, pl.ds(F, F // 2), pl.ds(k * NB, NB)], wsem.at[slot, 6 + k])
+            for k in range(2)]
+
+    def start_down(g, slot):
+        for c in down_copies(g, slot):
+            c.start()
+
+    def wait_down(g, slot):
+        for c in down_copies(g, slot):
+            c.wait()
 
     def own_block(t):
         return t - (T_OWN - T_P) * (t // T_OWN)
@@ -81,14 +95,14 @@
     def cols(n):
         return at(n * NB, NB)
 
-    def wide(n):
-        return at(n * 1024, 1024)
+    def tri(n):
+        return at(n * 3 * NB, 3 * NB)
 
     def dot(a, w):
         return jnp.dot(a, w, preferred_element_type=F32)
 
-    def own(rows, m, slot, i, halves=(0, 1)):
-        for b in halves:
+    def own(rows, m, slot, i):
+        for b in range(2):
             r = dot(X[pl.ds(rows, m), :], W[slot, :, pl.ds(b * 512, 512)])
             c = pl.ds(pl.multiple_of(i * 512 + b * 256, 256), 256)
             H[pl.ds(rows, m), c] = (jax.nn.silu(r[:, :256]) * r[:, 256:]).astype(BF)
@@ -151,18 +165,18 @@
 
     def far_copy(u, rows, dst, s, r, dev, go):
         if isinstance(u, int):
-            c = cols(u) if u < 2 else wide(u - 1)
+            c = cols(u) if u < 3 else tri(u - 2)
             go(rcopy(X.at[rows, c], dst.at[:, c], s.at[u], r.at[u], dev))
             return
 
-        @pl.when(u < 2)
+        @pl.when(u < 3)
         def _():
             c = cols(u)
             go(rcopy(X.at[rows, c], dst.at[:, c], s.at[u], r.at[u], dev))
 
-        @pl.when(u >= 2)
-        def _():
-            c = wide(u - 1)
+        @pl.when(u >= 3)
+        def _():
+            c = tri(u - 2)
             go(rcopy(X.at[rows, c], dst.at[:, c], s.at[u], r.at[u], dev))
 
     def send_d(u, go):
@@ -179,19 +193,25 @@
         return pl.ds(2 * R + n % 2 * R, R)
 
     def send_p(n):
-        return rcopy(X.at[pl.ds(0, R), wide(n)], H.at[landing(n), wide(n // 2)], qs.at[n], qr.at[n], partner)
+        return rcopy(X.at[pl.ds(0, R), tri(n)], H.at[landing(n), tri(n // 2)], qs.at[n], qr.at[n], partner)
 
     def pair_sum(c, h):
         X[pl.ds(3 * R, R), c] = (S[pl.ds(R, R), h] + rD[:, c].astype(F32)).astype(BF)
 
-    def down(rows, slot, w, keep_rows, keep, send_rows, c):
-        r = dot(H[pl.ds(rows, 2 * R), :], W[slot, pl.ds(0, F), w])
+    def down_dot(rows, m, slot, b):
+        if isinstance(b, int) and b == 2:
+            r = [dot(H[pl.ds(rows, m), pl.ds(k * F // 2, F // 2)],
+                     W[slot, pl.ds(F, F // 2), pl.ds(k * NB, NB)]) for k in range(2)]
+            return r[0] + r[1]
+        return dot(H[pl.ds(rows, m), :], W[slot, pl.ds(0, F), cols(b)])
+
+    def down(rows, slot, b, keep_rows, keep, send_rows, c):
+        r = down_dot(rows, 2 * R, slot, b)
         S[keep_rows, keep] = r[:R]
         X[send_rows, c] = r[R:].astype(BF)
 
     def step(t, carry):
-        late = t // (T_FAR + 1) - t // (2 * T_FAR + 2)
-        slot = lax.rem(t + late, 2)
+        slot = lax.rem(t, 2)
         other = 1 - slot
 
         @pl.when(t < T_FAR)
@@ -208,7 +228,7 @@
 
             @pl.when(t == T_FAR - 1)
             def _():
-                down_copy(0, other).start()
+                start_down(0, other)
 
             @pl.when((t == RELAY[0]) | (t == RELAY[1]) | (t == RELAY[2]) | (t == RELAY[3]))
             def _():
@@ -253,35 +273,25 @@
 
             @pl.when(u == 0)
             def _():
-                down_copy(1, other).start()
+                start_down(1, other)
                 for c in range(2):
                     to_partner(c).wait_send()
                 for k in range(NP):
                     to_remote(k).wait_send()
                     relay(k).wait_send()
 
-            @pl.when((u > 1) & (u < NU - 1))
-            def _():
-                down_copy(u, other).start()
-
-            @pl.when(u == NU - 2)
-            def _():
-                for c in own_copies(T_P, slot, rows=pl.ds(F, D - F)):
-                    c.start()
-
-            @pl.when(u == NU - 1)
-            def _():
-                for c in own_copies(T_P, other, rows=pl.ds(0, F)):
-                    c.start()
-
-            @pl.when((u >= NU) & (u < NU + 2))
+            @pl.when((u > 2) & (u < NU - 1))
+            def _():
+                start_down(u - 1, other)
+
+            @pl.when((u >= NU - 1) & (u < NU + 2))
             def _():
                 for c in own_copies(T_P + u - NU + 1, other):
                     c.start()
 
             @pl.when(u == NU + 2)
             def _():
-                down_copy(0, other).start()
+                start_down(0, other)
 
             @pl.when((u > 0) & (u <= NU))
             def _():
@@ -290,14 +300,21 @@
             @pl.when((u > 1) & (u <= NU + 1))
             def _():
                 send_r(u - 2, start)
+
+            def single(b):
+                down(2 * R, T_FAR % 2, b, pl.ds(R, R), cols(b), pl.ds(2 * R, R), cols(b))
 
             @pl.when(u < 2)
             def _():
                 @pl.when(u == 0)
                 def _():
-                    down_copy(0, T_FAR % 2).wait()
-
-                down(2 * R, T_FAR % 2, cols(u), pl.ds(R, R), cols(u), pl.ds(2 * R, R), cols(u))
+                    wait_down(0, T_FAR % 2)
+
+                single(u)
+
+            @pl.when(u == 2)
+            def _():
+                single(2)
 
         @pl.when((t < T_P) | ((t >= T_OWN) & (t < T_NEAR)))
         def _():
@@ -306,58 +323,54 @@
                 c.wait()
             own(0, 2 * R, slot, i)
 
-        @pl.when(((t >= T_FAR + 2) & (t < T_OWN)) | (t >= T_NEAR))
+        @pl.when(((t >= T_FAR + 3) & (t < T_OWN)) | (t >= T_NEAR))
         def _():
             near = t // T_NEAR
-            m = t - T_FAR - 1 - (T_NEAR - T_FAR - 1) * near
+            far = 1 - near
+            g = t - T_FAR - 2 - (T_NEAR - T_FAR - 2) * near
 
             @pl.when(t >= T_NEAR)
             def _():
-                down_copy(m + 1, other).start()
-
-            @pl.when((t >= T_NEAR) & (m > 0))
-            def _():
-                send_p(m - 1).start()
-
-            down_copy(m, slot).wait()
-            far = 1 - near
-            k = 2 * (lax.rem(m, 2) * far + m * near)
-            for b in range(2):
-                down(pl.multiple_of(2 * R * far, 128), slot, pl.ds(b * NB, NB),
+                start_down(g + 1, other)
+
+            @pl.when((t >= T_NEAR) & (g > 0))
+            def _():
+                send_p(g - 1).start()
+
+            wait_down(g, slot)
+            k = 3 * (lax.rem(g, 2) * far + g * near)
+            for b in range(3):
+                down(pl.multiple_of(2 * R * far, 128), slot, b,
                      pl.ds(pl.multiple_of(R * far, 64), R), cols(k + b),
-                     pl.ds(pl.multiple_of(2 * R * far, 128), R), cols(2 * m + b))
+                     pl.ds(pl.multiple_of(2 * R * far, 128), R), cols(3 * g + b))
 
         @pl.when((t > T_FAR) & (t <= T_OWN))
         def _():
             u = t - T_FAR - 1
             send_d(u, wait_recv)
 
-            @pl.when(u < 2)
+            @pl.when(u < 3)
             def _():
                 pair_sum(cols(u), cols(u))
 
-            @pl.when(u >= 2)
-            def _():
-                pair_sum(wide(u - 1), wide(lax.rem(u - 1, 2)))
+            @pl.when(u >= 3)
+            def _():
+                pair_sum(tri(u - 2), tri(lax.rem(u, 2)))
 
         return carry
 
     lax.fori_loop(1, T_END, step, 0)
 
-    last = ND // 2 - 1
+    last = NT - 1
 
     def arrived(n):
         send_p(n).wait_recv()
-        if n == 0:
-            send_r(0, wait_recv)
-        send_r(n + 1, wait_recv)
+        for u in (0, 1, 2) if n == 0 else (n + 2,):
+            send_r(u, wait_recv)
 
     def finish(n):
-        out[:, wide(n)] = (S[pl.ds(0, R), wide(n)] + H[landing(n), wide(n // 2)].astype(F32)
-                           + rR[:, wide(n)].astype(F32)).astype(BF)
-
-    def last_dot(rows, b):
-        return dot(H[pl.ds(rows, R), :], W[(T_END + 1) % 2, pl.ds(0, F), pl.ds(b * NB, NB)])
+        out[:, tri(n)] = (S[pl.ds(0, R), tri(n)] + H[landing(n), tri(n // 2)].astype(F32)
+                          + rR[:, tri(n)].astype(F32)).astype(BF)
 
     def drain(u, carry):
         send_d(u, wait_send)
@@ -365,12 +378,12 @@
         return carry
 
     send_p(last - 1).start()
-    down_copy(last, (T_END + 1) % 2).wait()
-    for b in range(2):
-        X[pl.ds(0, R), cols(2 * last + b)] = last_dot(R, b).astype(BF)
+    wait_down(last, T_END % 2)
+    for b in range(3):
+        X[pl.ds(0, R), cols(3 * last + b)] = down_dot(R, R, T_END % 2, b).astype(BF)
     send_p(last).start()
-    for b in range(2):
-        S[pl.ds(0, R), cols(2 * last + b)] = last_dot(0, b)
+    for b in range(3):
+        S[pl.ds(0, R), cols(3 * last + b)] = down_dot(0, R, T_END % 2, b)
     for n in range(last):
         arrived(n)
         finish(n)
@@ -406,7 +419,7 @@
                 dma((NP,)), dma((NP,)),
                 dma((NU,)), dma((NU,)),
                 dma((NU,)), dma((NU,)),
-                dma((ND // 2,)), dma((ND // 2,)),
+                dma((NT,)), dma((NT,)),
             ],
             compiler_params=pltpu.CompilerParams(
                 collective_id=0, has_side_effects=True, vmem_limit_bytes=64500000),

time: 134 us -> 133 us (level)
  no operation moved by 1% of the time
where the time goes in v7:
time: 133 us
  Pallas kernels  132 us (99%)
  local copies, waits for them, and re-layouts  1.41 us (1%)
    pallas_call x1, Pallas kernels, step(): pl.pallas_call(kernel, out_shape=pltpu.VMEM((R, D), BF), in_specs=[hbm] *...  132 us

profile of v7, /device:TPU:0, one launch (start us, length us, event | category | flops | bytes accessed | tf_op | source)
XLA Modules:
  0.0 133.3 jit_solution(15061942749978970037)
XLA Ops:
  0.0 131.9 %mlp.1 = bf16[192,6144]{1,0:T(8,128)(2,1)S(1)} custom-call(bf16[192,6144]{1,0:T(8,128)(2,1)} %x_hbm.1, bf16[6144,4096]{1,0:T(8,128)(2,1)} %wg.1, bf16[6144,4096]{1,0:T(8,128)(2,1)} %wu.1, bf16[4096,6144]{1,0:T(8,128)(2,1)} %wd.1), custom_call_target="tpu_custom_call" | custom-call | tf_op jit(solution)/shard_map/mlp/pallas_call | solution.py:403
  131.9 1.4 %copy.6 = bf16[192,6144]{1,0:T(8,128)(2,1)} copy(bf16[192,6144]{1,0:T(8,128)(2,1)S(1)} %mlp.1) | data formatting | bytes 4718592

commit v8 on v7

--- a/solution.py
+++ b/solution.py
@@ -262,10 +262,9 @@
                 @pl.when(p >= 2 * NP - 2)
                 def _():
                     for e in range(4):
-                        c, r = part(slot, p, e, 0)
-                        S[:, c] = jax.nn.silu(r)
+                        gate = jax.nn.silu(part(slot, p, e, 0)[1])
                         up = part(slot, p, e, 1)[1]
-                        H[pl.ds(2 * R, 2 * R), block(lax.rem(p, 2) * 4 + e)] = (S[:, c] * up).astype(BF)
+                        H[pl.ds(2 * R, 2 * R), block(lax.rem(p, 2) * 4 + e)] = (gate * up).astype(BF)
 
         @pl.when((t >= T_FAR) & (t < T_NEAR))
         def _():

time: 133 us -> 133 us (level)
  no operation moved by 1% of the time
where the time goes in v8:
time: 133 us
  Pallas kernels  132 us (99%)
  local copies, waits for them, and re-layouts  1.41 us (1%)
    pallas_call x1, Pallas kernels, step(): pl.pallas_call(kernel, out_shape=pltpu.VMEM((R, D), BF), in_specs=[hbm] *...  132 us

profile of v8, /device:TPU:0, one launch (start us, length us, event | category | flops | bytes accessed | tf_op | source)
XLA Modules:
  0.0 133.2 jit_solution(8565373529149989870)
XLA Ops:
  0.0 131.8 %mlp.1 = bf16[192,6144]{1,0:T(8,128)(2,1)S(1)} custom-call(bf16[192,6144]{1,0:T(8,128)(2,1)} %x_hbm.1, bf16[6144,4096]{1,0:T(8,128)(2,1)} %wg.1, bf16[6144,4096]{1,0:T(8,128)(2,1)} %wu.1, bf16[4096,6144]{1,0:T(8,128)(2,1)} %wd.1), custom_call_target="tpu_custom_call" | custom-call | tf_op jit(solution)/shard_map/mlp/pallas_call | solution.py:402
  131.8 1.4 %copy.6 = bf16[192,6144]{1,0:T(8,128)(2,1)} copy(bf16[192,6144]{1,0:T(8,128)(2,1)S(1)} %mlp.1) | data formatting | bytes 4718592
